TPU v7x, 32 devices: a whole 2x2x4 slice. The times are simulated.
32 devices in a mesh: dp: 4 (over x, core), expert: 4 (over z), etp: 2 (over y).
Axes of the slice: x: 2, y: 2, z: 4, core: 2. Of those that a mesh axis runs over, the one named last changes fastest.
Arguments:
- tokens: bfloat16 [4096, 3072], P(('dp', 'expert'), 'etp'), parts along dimension 0, may hold values from -6 to 6
- experts: int32 [4096, 2], P(('dp', 'expert')), parts along dimension 0, may hold values from 0 to 3, all different within a row; in each aligned block of 256 rows (0 to 255, 256 to 511, ...) at most 176 rows name the same one
- mixing: float32 [4096, 2], P(('dp', 'expert')), parts along dimension 0, may hold values from 0.2 to 1
- up_weight: bfloat16 [4, 3072, 8192], P('expert', None, 'etp'), may hold values from -0.109375 to 0.109375
- down_weight: bfloat16 [4, 8192, 3072], P('expert', 'etp'), may hold values from -0.0625 to 0.0625
Outputs:
- mixed: bfloat16 [4096, 3072], P(('dp', 'expert'), 'etp'), parts along dimension 0
There are 4 independent parts, one for each index of `dp`. A program takes and returns all parts, laid end to end along the dimension named above; an argument that names none is the same for every part. Nothing has to cross between parts.
Inputs may be any that keep to these rules, and one draw needn't show every extreme that they name: Each row names two different experts. In the rows of one index of expert (aligned blocks of 256 rows) no expert is named more than 176 times, a bound that some block reaches.
All inputs are finite; a program needn't handle non-finite values.
Results may differ from a plain program's by a relative error of at most 0.0078.
Values may be sent and summed in bfloat16 or wider, within the bound.
A program may use at most 128 MiB of HBM per device.

v0:
```python
import jax
import jax.numpy as jnp
from jax import lax
from jax.sharding import PartitionSpec as P


def slot_table(chosen, expert_count, capacity):
    flat_ids = chosen.reshape(-1)
    one_hot = (flat_ids[:, None] == jnp.arange(expert_count, dtype=jnp.int32)[None, :]).astype(
        jnp.int32
    )
    before = jnp.cumsum(one_hot, axis=0) - one_hot
    position = jnp.sum(before * one_hot, axis=1)
    return (flat_ids * capacity + position).reshape(chosen.shape)


def dispatch_rows(block_tokens, slot_ids, slot_total):
    one_hot = (
        slot_ids[:, :, None] == jnp.arange(slot_total, dtype=jnp.int32)[None, None, :]
    ).astype(jnp.bfloat16)
    placing = jnp.sum(one_hot, axis=1)
    return jnp.einsum(
        "rs,rd->sd", placing, block_tokens, preferred_element_type=jnp.float32
    ).astype(jnp.bfloat16)


def local(tokens, experts, mixing, up_weight, down_weight):
    tok_rows = experts.shape[0]
    part_width = tokens.shape[1]
    expert_count = up_weight.shape[0] * lax.axis_size("expert")
    capacity = 2 * tok_rows // expert_count * 11 // 8
    slot_total = expert_count * capacity
    up_slab = up_weight[0]
    down_slab = down_weight[0]
    slot_ids = slot_table(experts, expert_count, capacity)
    outgoing = dispatch_rows(tokens, slot_ids, slot_total).reshape(
        expert_count, capacity, part_width
    )
    arrived = lax.all_to_all(outgoing, "expert", split_axis=0, concat_axis=0, tiled=True)
    gathered = lax.all_gather(arrived.reshape(slot_total, part_width), "etp", axis=1, tiled=True)
    up_proj = jnp.dot(gathered, up_slab, preferred_element_type=jnp.float32)
    hidden = jax.nn.silu(up_proj).astype(jnp.bfloat16)
    partial_sums = jnp.dot(hidden, down_slab, preferred_element_type=jnp.float32)
    own_cols = lax.psum_scatter(partial_sums, "etp", scatter_dimension=1, tiled=True).astype(
        jnp.bfloat16
    )
    outputs = lax.all_to_all(
        own_cols.reshape(expert_count, capacity, part_width),
        "expert",
        split_axis=0,
        concat_axis=0,
        tiled=True,
    )
    flat_out = outputs.reshape(slot_total, part_width)
    picked = (
        jnp.take(flat_out, slot_ids.reshape(-1), axis=0)
        .reshape(tok_rows, 2, part_width)
        .astype(jnp.float32)
    )
    mixed = jnp.sum(picked * mixing[:, :, None], axis=1)
    return mixed.astype(jnp.bfloat16)


def solution(mesh):
    placed = (
        P(("dp", "expert"), "etp"),
        P(("dp", "expert"), None),
        P(("dp", "expert"), None),
        P("expert", None, "etp"),
        P("expert", "etp", None),
    )
    return jax.shard_map(
        local, mesh=mesh, in_specs=placed, out_specs=P(("dp", "expert"), "etp"), check_vma=False
    )
```

profile of v0, /device:TPU:0, one launch (start us, length us, event | category | flops | bytes accessed | tf_op | source)
XLA Modules:
  0.0 352.5 jit_solution(7086791842899878181)
XLA Ops:
  6.5 0.0 copy-start
  6.5 0.0 all-gather.2.cloned.1.call-start
  6.5 0.9 copy.18
  7.4 0.1 eq.39
  7.6 0.1 reshape.81
  7.7 1.2 reduce-window.6
  9.0 0.2 slice_reduce_fusion
  9.2 0.2 reduce-window.9
  9.4 0.1 add_bitcast_fusion
  9.5 0.1 reduce_sum.35
  9.6 0.1 copy.20
  9.7 0.7 compare_and_fusion
  10.4 0.3 fusion.10
  10.7 0.0 copy-done
  10.7 0.7 convolution_convert_fusion
  11.4 55.9 %all_to_all.10 = bf16[4,176,1536]{2,1,0:T(8,128)(2,1)} all-to-all(bf16[4,176,1536]{2,1,0:T(8,128)(2,1)S(1)} %bitcast.47), channel_id=1, replica_groups=mesh['dp'=4,'expert'=4,'etp'=2] {'expert'}, dimensions={0} | all-to-all | bytes 4325376 | tf_op jit(solution)/shard_map/all_to_all | solution.py:39
  67.3 0.0 all-gather.2.cloned.1.call-update
  67.3 0.0 reduce-scatter.2.cloned.1.call-start
  67.4 57.5 %all-gather.2.cloned.1.call-done = bf16[704,3072]{1,0:T(8,128)(2,1)} async-done(((bf16[704,1536]{1,0:T(8,128)(2,1)}), bf16[704,3072]{1,0:T(8,128)(2,1)}) %all-gather.2.cloned.1.call-update) | async-done | bytes 4325392 | tf_op jit(solution)/shard_map/all_gather | solution.py:40
  124.9 23.9 %multiply_convert_fusion.4 = bf16[704,4096]{1,0:T(8,128)(2,1)S(1)} fusion(bf16[704,3072]{1,0:T(8,128)(2,1)} %all-gather.2.cloned.1.call-done, bf16[1,3072,4096]{2,1,0:T(8,128)(2,1)} %param.8), kind=kOutput, calls=%fused_computation.5.clone.clone.1 | convolution fusion | flops 17731158016 | bytes 35258368 | tf_op jit(solution)/shard_map/dot_general | solution.py:41
  148.8 22.8 %fusion = f32[704,3072]{1,0:T(8,128)} fusion(bf16[1,4096,3072]{2,1,0:T(8,128)(2,1)} %param.9, bf16[704,4096]{1,0:T(8,128)(2,1)S(1)} %multiply_convert_fusion.4), kind=kOutput, calls=%fused_computation.1 | convolution fusion | flops 17716740096 | bytes 39583744 | tf_op jit(solution)/shard_map/dot_general | solution.py:43
  171.6 0.0 reduce-scatter.2.cloned.1.call-update
  171.6 0.0 copy-start.2
  171.6 0.0 copy-start.3
  171.6 102.3 %reduce-scatter.2.cloned.1.call-done = f32[704,1536]{1,0:T(8,128)} async-done(((f32[704,3072]{1,0:T(8,128)}), f32[704,1536]{1,0:T(8,128)}) %reduce-scatter.2.cloned.1.call-update) | async-done | bytes 4325392 | tf_op jit(solution)/shard_map/reduce_scatter | solution.py:44
  273.9 3.8 %convert_element_type.32 = bf16[704,1536]{1,0:T(8,128)(2,1)} convert(f32[704,1536]{1,0:T(8,128)} %reduce-scatter.2.cloned.1.call-done) | non-fusion elementwise | flops 1081344 | bytes 6488064 | tf_op jit(solution)/shard_map/convert_element_type | solution.py:44
  277.7 4.6 %all-to-all-start.1 = ((bf16[4,176,1536]{2,1,0:T(8,128)(2,1)}), bf16[4,176,1536]{2,1,0:T(8,128)(2,1)S(1)}, u32[]{:S(2)}, u32[]{:S(2)}) async-start(bf16[4,176,1536]{2,1,0:T(8,128)(2,1)} %bitcast.48), calls=%async_computation.2 | async-start | bytes 4325376 | tf_op jit(solution)/shard_map/all_to_all | solution.py:47
  282.4 0.0 copy-done.2
  282.4 0.1 copy.22
  282.5 0.1 mul.40
  282.7 0.2 copy.21
  282.8 0.0 copy-done.3
  282.9 0.1 copy.23
  283.0 48.8 %all-to-all-done.1 = bf16[4,176,1536]{2,1,0:T(8,128)(2,1)S(1)} async-done(((bf16[4,176,1536]{2,1,0:T(8,128)(2,1)}), bf16[4,176,1536]{2,1,0:T(8,128)(2,1)S(1)}, u32[]{:S(2)}, u32[]{:S(2)}) %all-to-all-start.1) | async-done | bytes 2162720 | tf_op jit(solution)/shard_map/all_to_all | solution.py:47
  331.8 0.0 copy-start.1
  331.8 3.0 gather_fusion
  334.8 3.5 gather.7
  338.3 7.4 %multiply_reduce_fusion = bf16[256,1536]{1,0:T(8,128)(2,1)} fusion(bf16[256,2,1536]{2,1,0:T(2,128)(2,1)S(1)} %gather.7, pred[256,2]{1,0:T(8,128)(4,1)S(1)} %copy.21, f32[256,2]{1,0:T(8,128)S(1)} %copy.23), kind=kLoop, calls=%fused_computation.8 | loop fusion | flops 2752512 | bytes 2361856 | tf_op jit(solution)/shard_map/reduce_sum | solution.py:60
  345.7 0.0 copy-done.1
  (5 shorter events, 0.0 us)
Async XLA Ops:
  6.5 4.2 %copy-start = (bf16[256,1536]{1,0:T(8,128)(2,1)S(1)}, bf16[256,1536]{1,0:T(8,128)(2,1)}, u32[]{:S(2)}) copy-start(bf16[256,1536]{1,0:T(8,128)(2,1)} %param.5) | copy-start | bytes 2359300
  6.5 118.4 %all-gather.2.cloned.1.call-start = ((), (), s32[]{:S(2)}) async-start(), calls=%async_computation.3 | async-start | bytes 6488064 | tf_op jit(solution)/shard_map/all_gather | solution.py:40
  67.3 206.6 %reduce-scatter.2.cloned.1.call-start = ((), (), s32[]{:S(2)}) async-start(), calls=%async_computation.4 | async-start | bytes 12976128 | tf_op jit(solution)/shard_map/reduce_scatter | solution.py:44
  171.6 110.7 %copy-start.2 = (s32[256,2]{0,1:T(2,128)S(1)}, s32[256,2]{0,1:T(2,128)}, u32[]{:S(2)}) copy-start(s32[256,2]{0,1:T(2,128)} %param.6) | copy-start | bytes 6148
  171.6 111.2 %copy-start.3 = (f32[256,2]{0,1:T(2,128)S(1)}, f32[256,2]{0,1:T(2,128)}, u32[]{:S(2)}) copy-start(f32[256,2]{0,1:T(2,128)} %param.7) | copy-start | bytes 6148
  277.7 54.1 %all-to-all-start.1 = ((bf16[4,176,1536]{2,1,0:T(8,128)(2,1)}), bf16[4,176,1536]{2,1,0:T(8,128)(2,1)S(1)}, u32[]{:S(2)}, u32[]{:S(2)}) async-start(bf16[4,176,1536]{2,1,0:T(8,128)(2,1)} %bitcast.48), calls=%async_computation.2 | async-start | bytes 4325376 | tf_op jit(solution)/shard_map/all_to_all | solution.py:47
  331.8 13.9 %copy-start.1 = (bf16[256,1536]{1,0:T(8,128)(2,1)S(1)}, bf16[256,1536]{1,0:T(8,128)(2,1)}, u32[]{:S(2)}) copy-start(bf16[256,1536]{1,0:T(8,128)(2,1)} %param.5) | copy-start | bytes 2359300
Sparse Core Ops, SparseCore 0:
  67.4 57.4 all-gather.1
  171.7 102.1 reduce-scatter.1
where the time goes:
time: 353 us
  waiting for transfers between devices  209 us (59%)
  blocking collectives  55.9 us (16%)
  matrix products  47.4 us (13%)
  other arithmetic  13.8 us (4%)
  between operations  13.5 us (4%)
  local copies, waits for them, and re-layouts  8.66 us (2%)
  starting transfers between devices  4.67 us (1%)
    reduce_scatter x1, waiting for transfers between devices, local(): lax.psum_scatter(partial_sums, 'etp', scatter_dimension=1, tiled=True)  102 us
    all_gather x1, waiting for transfers between devices, local(): lax.all_gather(arrived.reshape(slot_total, part_width), 'etp', axis=1, ti...  57.5 us
    all_to_all x1, blocking collectives, local(): lax.all_to_all(outgoing, 'expert', split_axis=0, concat_axis=0, tiled=True)  55.9 us
    all_to_all x1, waiting for transfers between devices, local(): lax.all_to_all(own_cols.reshape(expert_count, capacity, part_width), 'exp...  48.8 us
    dot_general x1, matrix products, local(): up_proj = jnp.dot(gathered, up_slab, preferred_element_type=jnp.float32)  23.9 us
    dot_general x1, matrix products, local(): jnp.dot(hidden, down_slab, preferred_element_type=jnp.float32)  22.8 us
    reduce_sum x1, other arithmetic, local(): mixed = jnp.sum(picked * mixing[:, :, None], axis=1)  7.44 us
  transfers between devices with their start and end apart: 3, of which 3 were waited for; matrix products, arithmetic and copies ran while one was open for 0% of the time, Pallas kernels for 0%

commit v1 on v0

--- a/solution.py
+++ b/solution.py
@@ -2,6 +2,18 @@
 import jax.numpy as jnp
 from jax import lax
 from jax.sharding import PartitionSpec as P
+
+
+def gather_by_bits(x, axis, dim):
+    ways, here, lap = (lax.axis_size(axis), lax.axis_index(axis), x.shape[dim])
+    line, have = (x, 1)
+    while have < ways:
+        line = jnp.concatenate(
+            [line, lax.ppermute(line, axis, [(d, (d - have) % ways) for d in range(ways)])],
+            axis=dim,
+        )
+        have = 2 * have
+    return jnp.roll(line, here * lap, axis=dim)
 
 
 def slot_table(chosen, expert_count, capacity):
@@ -37,7 +49,7 @@
         expert_count, capacity, part_width
     )
     arrived = lax.all_to_all(outgoing, "expert", split_axis=0, concat_axis=0, tiled=True)
-    gathered = lax.all_gather(arrived.reshape(slot_total, part_width), "etp", axis=1, tiled=True)
+    gathered = gather_by_bits(arrived.reshape(slot_total, part_width), "etp", 1)
     up_proj = jnp.dot(gathered, up_slab, preferred_element_type=jnp.float32)
     hidden = jax.nn.silu(up_proj).astype(jnp.bfloat16)
     partial_sums = jnp.dot(hidden, down_slab, preferred_element_type=jnp.float32)

time: 353 us -> 353 us (level)
  waiting for transfers between devices: 209 us -> 197 us
  matrix products: 47.4 us -> 57.7 us
    all_gather x1 -> x0, waiting for transfers between devices: 57.5 us -> none  [local(): lax.all_gather(arrived.reshape(slot_total, part_width), 'etp', axis=1, ti...]
    ppermute x0 -> x1, waiting for transfers between devices: none -> 46.6 us  [gather_by_bits(): lax.ppermute(line, axis, [(d, (d - have) % ways) for d in range(ways)])]
    dot_general x1, matrix products: 23.9 us -> 32.6 us  [local(): up_proj = jnp.dot(gathered, up_slab, preferred_element_type=jnp.float32)]
where the time goes in v1:
time: 353 us; the launch traced here: 352 us
  waiting for transfers between devices  197 us (56%)
  matrix products  57.7 us (16%)
  blocking collectives  55.7 us (16%)
  other arithmetic  13.8 us (4%)
  between operations  13.5 us (4%)
  local copies, waits for them, and re-layouts  8.66 us (2%)
  starting transfers between devices  6.13 us (2%)
    reduce_scatter x1, waiting for transfers between devices, local(): lax.psum_scatter(partial_sums, 'etp', scatter_dimension=1, tiled=True)  101 us
    all_to_all x1, blocking collectives, local(): lax.all_to_all(outgoing, 'expert', split_axis=0, concat_axis=0, tiled=True)  55.7 us
    all_to_all x1, waiting for transfers between devices, local(): lax.all_to_all(own_cols.reshape(expert_count, capacity, part_width), 'exp...  48.8 us
    ppermute x1, waiting for transfers between devices, gather_by_bits(): lax.ppermute(line, axis, [(d, (d - have) % ways) for d in range(ways)])  46.6 us
    dot_general x1, matrix products, local(): up_proj = jnp.dot(gathered, up_slab, preferred_element_type=jnp.float32)  32.6 us
    dot_general x1, matrix products, local(): jnp.dot(hidden, down_slab, preferred_element_type=jnp.float32)  24.4 us
    reduce_sum x1, other arithmetic, local(): mixed = jnp.sum(picked * mixing[:, :, None], axis=1)  7.44 us
  transfers between devices with their start and end apart: 3, of which 3 were waited for; matrix products, arithmetic and copies ran while one was open for 0% of the time, Pallas kernels for 0%

profile of v1, /device:TPU:0, one launch (start us, length us, event | category | flops | bytes accessed | tf_op | source)
XLA Modules:
  0.0 352.4 jit_solution(12369411550982560324)
XLA Ops:
  6.5 0.0 copy-start
  6.5 0.0 reduce-scatter.2.cloned.1.call-start
  6.5 0.9 copy.18
  7.4 0.1 eq.42
  7.6 0.1 reshape.81
  7.7 1.2 reduce-window.6
  9.0 0.2 slice_reduce_fusion
  9.2 0.2 reduce-window.9
  9.4 0.1 add_bitcast_fusion
  9.5 0.1 reduce_sum.35
  9.6 0.1 copy.20
  9.7 0.7 compare_and_fusion
  10.4 0.3 fusion.15
  10.7 0.0 copy-done
  10.7 0.7 convolution_convert_fusion
  11.4 55.7 %all_to_all.10 = bf16[4,176,1536]{2,1,0:T(8,128)(2,1)S(1)} all-to-all(bf16[4,176,1536]{2,1,0:T(8,128)(2,1)S(1)} %bitcast.43), channel_id=1, replica_groups=mesh['dp'=4,'expert'=4,'etp'=2] {'expert'}, dimensions={0} | all-to-all | bytes 4325376 | tf_op jit(solution)/shard_map/all_to_all | solution.py:51
  67.2 1.5 collective-permute-start
  68.7 46.6 %collective-permute-done = bf16[704,1536]{1,0:T(8,128)(2,1)} collective-permute-done((bf16[704,1536]{1,0:T(8,128)(2,1)S(1)}, bf16[704,1536]{1,0:T(8,128)(2,1)}, u32[]{:S(2)}, u32[]{:S(2)}) %collective-permute-start) | collective-permute-done | bytes 2162720 | tf_op jit(solution)/shard_map/ppermute | solution.py:12
  115.3 32.6 %multiply_convert_fusion.4 = bf16[704,4096]{1,0:T(8,128)(2,1)} fusion(bf16[1,3072,4096]{2,1,0:T(8,128)(2,1)} %param.8, s32[]{:T(128)S(6)} %select_n.37, bf16[704,1536]{1,0:T(8,128)(2,1)S(1)} %bitcast.46, bf16[704,1536]{1,0:T(8,128)(2,1)} %collective-permute-done), kind=kOutput, calls=%fused_computation.5.clone.clone.1 | convolution fusion | flops 17748459520 | bytes 35258372 | tf_op jit(solution)/shard_map/dot_general | solution.py:53
  147.8 24.4 %fusion = f32[704,3072]{1,0:T(8,128)} fusion(bf16[1,4096,3072]{2,1,0:T(8,128)(2,1)} %param.9, bf16[704,4096]{1,0:T(8,128)(2,1)} %multiply_convert_fusion.4), kind=kOutput, calls=%fused_computation.1 | convolution fusion | flops 17716740096 | bytes 39583744 | tf_op jit(solution)/shard_map/dot_general | solution.py:55
  172.2 0.0 reduce-scatter.2.cloned.1.call-update
  172.3 0.0 copy-start.2
  172.3 0.0 copy-start.3
  172.3 101.5 %reduce-scatter.2.cloned.1.call-done = f32[704,1536]{1,0:T(8,128)} async-done(((f32[704,3072]{1,0:T(8,128)}), f32[704,1536]{1,0:T(8,128)}) %reduce-scatter.2.cloned.1.call-update) | async-done | bytes 4325392 | tf_op jit(solution)/shard_map/reduce_scatter | solution.py:56
  273.8 3.8 %convert_element_type.32 = bf16[704,1536]{1,0:T(8,128)(2,1)} convert(f32[704,1536]{1,0:T(8,128)} %reduce-scatter.2.cloned.1.call-done) | non-fusion elementwise | flops 1081344 | bytes 6488064 | tf_op jit(solution)/shard_map/convert_element_type | solution.py:56
  277.6 4.6 %all-to-all-start.1 = ((bf16[4,176,1536]{2,1,0:T(8,128)(2,1)}), bf16[4,176,1536]{2,1,0:T(8,128)(2,1)S(1)}, u32[]{:S(2)}, u32[]{:S(2)}) async-start(bf16[4,176,1536]{2,1,0:T(8,128)(2,1)} %bitcast.44), calls=%async_computation.2 | async-start | bytes 4325376 | tf_op jit(solution)/shard_map/all_to_all | solution.py:59
  282.2 0.0 copy-done.2
  282.2 0.1 copy.22
  282.3 0.1 mul.44
  282.5 0.2 copy.21
  282.7 0.0 copy-done.3
  282.7 0.1 copy.23
  282.8 48.8 %all-to-all-done.1 = bf16[4,176,1536]{2,1,0:T(8,128)(2,1)S(1)} async-done(((bf16[4,176,1536]{2,1,0:T(8,128)(2,1)}), bf16[4,176,1536]{2,1,0:T(8,128)(2,1)S(1)}, u32[]{:S(2)}, u32[]{:S(2)}) %all-to-all-start.1) | async-done | bytes 2162720 | tf_op jit(solution)/shard_map/all_to_all | solution.py:59
  331.6 0.0 copy-start.1
  331.6 3.0 gather_fusion
  334.6 3.5 gather.7
  338.1 7.4 %multiply_reduce_fusion = bf16[256,1536]{1,0:T(8,128)(2,1)} fusion(bf16[256,2,1536]{2,1,0:T(2,128)(2,1)S(1)} %gather.7, pred[256,2]{1,0:T(8,128)(4,1)S(1)} %copy.21, f32[256,2]{1,0:T(8,128)S(1)} %copy.23), kind=kLoop, calls=%fused_computation.15 | loop fusion | flops 2752512 | bytes 2361856 | tf_op jit(solution)/shard_map/reduce_sum | solution.py:72
  345.5 0.0 copy-done.1
  (5 shorter events, 0.0 us)
Async XLA Ops:
  6.5 4.2 %copy-start = (bf16[256,1536]{1,0:T(8,128)(2,1)S(1)}, bf16[256,1536]{1,0:T(8,128)(2,1)}, u32[]{:S(2)}) copy-start(bf16[256,1536]{1,0:T(8,128)(2,1)} %param.5) | copy-start | bytes 2359300
  6.5 267.2 %reduce-scatter.2.cloned.1.call-start = ((), (), s32[]{:S(2)}) async-start(), calls=%async_computation.3 | async-start | bytes 12976128 | tf_op jit(solution)/shard_map/reduce_scatter | solution.py:56
  67.2 48.1 %collective-permute-start = (bf16[704,1536]{1,0:T(8,128)(2,1)S(1)}, bf16[704,1536]{1,0:T(8,128)(2,1)}, u32[]{:S(2)}, u32[]{:S(2)}) collective-permute-start(bf16[704,1536]{1,0:T(8,128)(2,1)S(1)} %bitcast.45), channel_id=1, source_target_pairs={{0,1},{1,0},{2,3},{3,2},{4,5},{5,4},{6,7},{7,6},{8,9},{9,8},{10,11... | collective-permute-start | bytes 6488072 | tf_op jit(solution)/shard_map/ppermute | solution.py:12
  172.3 109.9 %copy-start.2 = (s32[256,2]{0,1:T(2,128)S(1)}, s32[256,2]{0,1:T(2,128)}, u32[]{:S(2)}) copy-start(s32[256,2]{0,1:T(2,128)} %param.6) | copy-start | bytes 6148
  172.3 110.4 %copy-start.3 = (f32[256,2]{0,1:T(2,128)S(1)}, f32[256,2]{0,1:T(2,128)}, u32[]{:S(2)}) copy-start(f32[256,2]{0,1:T(2,128)} %param.7) | copy-start | bytes 6148
  277.6 54.0 %all-to-all-start.1 = ((bf16[4,176,1536]{2,1,0:T(8,128)(2,1)}), bf16[4,176,1536]{2,1,0:T(8,128)(2,1)S(1)}, u32[]{:S(2)}, u32[]{:S(2)}) async-start(bf16[4,176,1536]{2,1,0:T(8,128)(2,1)} %bitcast.44), calls=%async_computation.2 | async-start | bytes 4325376 | tf_op jit(solution)/shard_map/all_to_all | solution.py:59
  331.6 13.9 %copy-start.1 = (bf16[256,1536]{1,0:T(8,128)(2,1)S(1)}, bf16[256,1536]{1,0:T(8,128)(2,1)}, u32[]{:S(2)}) copy-start(bf16[256,1536]{1,0:T(8,128)(2,1)} %param.5) | copy-start | bytes 2359300
Sparse Core Ops, SparseCore 0:
  172.4 101.3 reduce-scatter.1
